TPU v7x, 32 devices: a whole 2x2x4 slice. The times are simulated.
32 devices in a mesh: outer: 4 (over y, core), inner: 8 (over z, x).
Axes of the slice: x: 2, y: 2, z: 4, core: 2. Of those that a mesh axis runs over, the one named last changes fastest.
Arguments:
- tokens: bfloat16 [12288, 4096], P(('outer', 'inner')), may hold values from -6 to 6
- out_grad: bfloat16 [12288, 1024], P(('outer', 'inner')), may hold values from -0.3125 to 0.3125
- master_weights: float32 [1024, 4096], P(('outer', 'inner')), may hold values from -0.0421 to 0.0421
- base_weights: bfloat16 [1024, 4096], replicated, may hold values from -0.030029297 to 0.030029297
- adam_m: float32 [1024, 4096], P(('outer', 'inner')), may hold values from -8 to 8
- adam_v: float32 [1024, 4096], P(('outer', 'inner')), may hold values from 0.1 to 10
- grad_exps: int32 [32, 8, 32], P(('outer', 'inner')), may hold values from -13 to -8
- diff_exps: int32 [1024, 32], P(('outer', 'inner')), may hold values from -20 to -15
- hadamard_signs: int32 [32, 128], replicated, may hold values 0 or 1
Outputs:
- projected: bfloat16 [12288, 1024], P(('outer', 'inner'))
- new_master: float32 [1024, 4096], P(('outer', 'inner'))
- new_first: float32 [1024, 4096], P(('outer', 'inner'))
- new_second: float32 [1024, 4096], P(('outer', 'inner'))
All inputs are finite; a program needn't handle non-finite values.
Results may differ from a plain program's by a relative error of at most 0.005.
Values may be sent and summed in bfloat16 or wider, within the bound.
A program may use at most 128 MiB of HBM per device.

v0:
```python
import math

import jax
import jax.numpy as jnp
from jax import lax
from jax.sharding import PartitionSpec as P

ADAM_STEP = 10


clip_level = 448.0
beta_one = 0.9
beta_two = 0.95
learn_rate = 0.002
decay_rate = 0.1
adam_eps = 1e-08
highest = lax.Precision.HIGHEST


def hadamard(matrix_size):
    positions = jnp.arange(matrix_size, dtype=jnp.int32)
    common = positions[:, None] & positions[None, :]
    parity = jnp.zeros((matrix_size, matrix_size), jnp.int32)
    for bit_level in range(matrix_size.bit_length() - 1):
        parity = parity + (common >> bit_level & 1)
    return (1 - 2 * (parity % 2)).astype(jnp.float32)


def rotate_rows(row_block, sign_rows, matrix):
    row_count = row_block.shape[0]
    blocks = row_block.reshape(row_count, sign_rows.shape[0], sign_rows.shape[1]) * sign_rows
    turned = jnp.dot(blocks.reshape(-1, sign_rows.shape[1]), matrix, precision=highest)
    return turned.reshape(row_block.shape) / math.sqrt(sign_rows.shape[1])


def unrotate_rows(row_block, sign_rows, matrix):
    row_count = row_block.shape[0]
    turned = jnp.dot(
        row_block.reshape(-1, sign_rows.shape[1]), matrix, precision=highest
    ) / math.sqrt(sign_rows.shape[1])
    return (turned.reshape(row_count, sign_rows.shape[0], sign_rows.shape[1]) * sign_rows).reshape(
        row_block.shape
    )


def clip_rows(row_block, bound_rows):
    row_count = row_block.shape[0]
    shaped = row_block.reshape(row_count, bound_rows.shape[1], -1)
    limits = bound_rows[:, :, None]
    return jnp.clip(shaped, -limits, limits).reshape(row_block.shape)


def adam_update(gradient, master, first, second):
    new_first = beta_one * first + (1.0 - beta_one) * gradient
    new_second = beta_two * second + (1.0 - beta_two) * gradient * gradient
    fix_one = 1.0 - beta_one**ADAM_STEP
    fix_two = 1.0 - beta_two**ADAM_STEP
    step_dir = new_first / fix_one / (jnp.sqrt(new_second / fix_two) + adam_eps)
    new_master = master - learn_rate * (step_dir + decay_rate * master)
    return (new_master, new_first, new_second)


def shards(
    tokens,
    out_grad,
    master_weights,
    base_weights,
    adam_m,
    adam_v,
    grad_exps,
    diff_exps,
    hadamard_signs,
):
    outer_count = lax.axis_size("outer")
    inner_count = lax.axis_size("inner")
    token_rows = tokens.shape[0]
    model_width = tokens.shape[1]
    rows_dev = master_weights.shape[0]
    sign_rows = (2 * hadamard_signs - 1).astype(jnp.float32)
    block_len = sign_rows.shape[1]
    col_blocks = sign_rows.shape[0]
    matrix = hadamard(block_len)
    bound_all = jnp.repeat(
        clip_level * jnp.exp2(grad_exps[0].astype(jnp.float32)), block_len, axis=0
    )
    grad_grid = out_grad.reshape(token_rows, outer_count, inner_count, rows_dev).transpose(
        0, 2, 1, 3
    )
    bound_grid = bound_all.reshape(outer_count, inner_count, rows_dev, col_blocks).transpose(
        1, 0, 2, 3
    )
    coded_bound_sel = bound_grid.reshape(-1, col_blocks)
    term_rows = lax.dot_general(
        grad_grid.reshape(token_rows, -1),
        tokens,
        (((0,), (0,)), ((), ())),
        preferred_element_type=jnp.float32,
    )
    turned = rotate_rows(term_rows, sign_rows, matrix)
    coded_rows = lax.optimization_barrier(clip_rows(turned, coded_bound_sel).astype(jnp.bfloat16))
    coded_rows = coded_rows.astype(jnp.float32)
    group_sum = lax.psum_scatter(
        coded_rows.reshape(1 * lax.axis_size("inner"), outer_count, rows_dev, model_width).astype(
            jnp.bfloat16
        ),
        "inner",
        scatter_dimension=0,
        tiled=True,
    )
    summed = (
        lax.psum_scatter(group_sum, "outer", scatter_dimension=1, tiled=True)
        .astype(jnp.float32)
        .reshape(rows_dev, model_width)
    )
    gradient = unrotate_rows(summed, sign_rows, matrix)
    new_master, new_first, new_second = adam_update(gradient, master_weights, adam_m, adam_v)
    owner = lax.axis_index("outer") * inner_count + lax.axis_index("inner")
    base_own = lax.dynamic_slice_in_dim(base_weights, owner * rows_dev, rows_dev, 0).astype(
        jnp.float32
    )
    diff_bound = clip_level * jnp.exp2(diff_exps.astype(jnp.float32))
    diff_coded = clip_rows(new_master - base_own, diff_bound).astype(jnp.bfloat16)
    effective = (
        base_weights.astype(jnp.float32)
        + lax.all_gather(diff_coded, ("outer", "inner"), axis=0, tiled=True).astype(jnp.float32)
    ).astype(jnp.bfloat16)
    result = lax.dot_general(
        tokens, effective, (((1,), (1,)), ((), ())), preferred_element_type=jnp.float32
    )
    projected = result.astype(jnp.bfloat16)
    return (projected, new_master, new_first, new_second)


def solution(mesh):
    in_specs = (
        P(("outer", "inner"), None),
        P(("outer", "inner"), None),
        P(("outer", "inner"), None),
        P(),
        P(("outer", "inner"), None),
        P(("outer", "inner"), None),
        P(("outer", "inner"), None, None),
        P(("outer", "inner"), None),
        P(),
    )
    out_specs = (
        P(("outer", "inner"), None),
        P(("outer", "inner"), None),
        P(("outer", "inner"), None),
        P(("outer", "inner"), None),
    )
    return jax.shard_map(shards, mesh=mesh, in_specs=in_specs, out_specs=out_specs, check_vma=False)
```

profile of v0, /device:TPU:0, one launch (start us, length us, event | category | flops | bytes accessed | tf_op | source)
XLA Modules:
  0.0 378.7 jit_solution(1837191897619309702)
XLA Ops:
  7.2 0.0 reduce-scatter.3.cloned.1.call-start
  7.2 0.7 fusion.28
  7.9 3.4 copy.27
  11.4 2.3 copy.22
  13.6 1.2 copy.23
  14.9 4.6 %convolution_multiply_fusion.1 = f32[1024,32,128]{2,0,1:T(8,128)S(1)} fusion(bf16[384,1024,1]{0,1,2:T(8,128)(2,1)S(1)} %bitcast.55, bf16[32,128,384]{2,1,0:T(8,128)(2,1)S(1)} %bitcast.54, f32[32,128]{1,0:T(8,128)S(1)} %get-tuple-element.21), kind=kOutput, calls=%fused_computation.5 | convolution fusion | flops 3225419776 | bytes 20725760 | tf_op jit(solution)/shard_map/dot_general | solution.py:93
  19.5 20.2 %copy.25 = f32[1024,32,128]{2,1,0:T(8,128)S(1)} copy(f32[1024,32,128]{2,0,1:T(8,128)S(1)} %convolution_multiply_fusion.1) | data formatting | bytes 33554432 | tf_op jit(solution)/shard_map/mul | solution.py:31
  39.7 15.3 %convolution_multiply_fusion = bf16[32768,128]{1,0:T(8,128)(2,1)} fusion(f32[32768,128]{1,0:T(8,128)S(1)} %bitcast.48), kind=kOutput, calls=%fused_computation | convolution fusion | flops 6451412992 | bytes 25165824 | tf_op jit(solution)/shard_map/dot_general | solution.py:32
  55.0 0.0 copy-start.2
  55.0 13.3 %div.31 = bf16[1024,4096]{1,0:T(8,128)(2,1)} reshape(bf16[32768,128]{1,0:T(8,128)(2,1)} %convolution_multiply_fusion) | data formatting | bytes 16777216 | tf_op jit(solution)/shard_map/div | solution.py:33
  68.3 0.0 copy-done.2
  68.4 0.0 slice-start
  68.4 11.7 %min.35 = bf16[1024,32,128]{2,1,0:T(8,128)(2,1)S(1)} broadcast(bf16[1024,32]{1,0:T(8,128)(2,1)S(1)} %bitcast.60), dimensions={0,1} | broadcast | bytes 8454144 | tf_op jit(solution)/shard_map/jit(clip)/min | solution.py:50
  80.2 0.0 slice-start.1
  80.2 11.7 %max.32 = bf16[1024,32,128]{2,1,0:T(8,128)(2,1)S(1)} broadcast(bf16[1024,32]{1,0:T(8,128)(2,1)S(1)} %bitcast_negate_fusion), dimensions={0,1} | broadcast | bytes 8454144 | tf_op jit(solution)/shard_map/jit(clip)/max | solution.py:50
  91.9 0.0 slice-done
  91.9 0.0 slice-done.1
  91.9 6.7 %fusion.1 = bf16[1024,4096]{1,0:T(8,128)(2,1)} fusion(bf16[1024,4096]{1,0:T(8,128)(2,1)S(1)} %bitcast.50, bf16[128,8,32,128]{3,2,1,0:T(8,128)(2,1)S(1)} %bitcast.53, bf16[128,8,32,128]{3,2,1,0:T(8,128)(2,1)S(1)} %bitcast.52), kind=kLoop, calls=%fused_computation.3 | loop fusion | flops 8388608 | bytes 33554432 | tf_op jit(solution)/shard_map/convert_element_type | solution.py:100
  98.6 0.0 copy-start.1
  98.6 0.0 copy-start
  98.6 0.0 reduce-scatter.3.cloned.1.call-update
  98.6 0.0 reduce-scatter.5.cloned.1.call-start
  98.7 150.3 %reduce-scatter.3.cloned.1.call-done = bf16[1,4,32,4096]{3,2,1,0:T(8,128)(2,1)} async-done(((bf16[8,4,32,4096]{3,2,1,0:T(8,128)(2,1)}), bf16[1,4,32,4096]{3,2,1,0:T(8,128)(2,1)}) %reduce-scatter.3.cloned.1.call-update) | async-done | bytes 1048592 | tf_op jit(solution)/shard_map/reduce_scatter | solution.py:102
  249.0 0.0 reduce-scatter.5.cloned.1.call-update
  249.0 0.0 all-gather.2.cloned.1.call-start
  249.1 0.0 copy-done.1
  249.1 26.3 %reduce-scatter.5.cloned.1.call-done = bf16[1,1,32,4096]{3,2,1,0:T(8,128)(2,1)} async-done(((bf16[1,4,32,4096]{3,2,1,0:T(8,128)(2,1)}), bf16[1,1,32,4096]{3,2,1,0:T(8,128)(2,1)}) %reduce-scatter.5.cloned.1.call-update) | async-done | bytes 262160 | tf_op jit(solution)/shard_map/reduce_scatter | solution.py:111
  275.4 1.1 reshape_reshape.4
  276.5 1.2 convolution_multiply_fusion.2
  277.7 1.9 reshape.62
  279.7 0.2 min.32
  279.9 0.2 max.30
  280.1 3.2 fusion.7
  283.3 0.0 all-gather.2.cloned.1.call-update
  283.4 77.2 %all-gather.2.cloned.1.call-done = bf16[1024,4096]{1,0:T(8,128)(2,1)} async-done(((bf16[32,4096]{1,0:T(8,128)(2,1)}), bf16[1024,4096]{1,0:T(8,128)(2,1)}) %all-gather.2.cloned.1.call-update) | async-done | bytes 8388624 | tf_op jit(solution)/shard_map/all_gather | solution.py:125
  360.6 0.0 copy-done
  360.6 9.2 %fusion.4 = bf16[384,1024]{0,1:T(8,128)(2,1)} fusion(bf16[384,4096]{1,0:T(8,128)(2,1)S(1)} %copy-done, bf16[1024,4096]{1,0:T(8,128)(2,1)} %all-gather.2.cloned.1.call-done, bf16[1024,4096]{1,0:T(8,128)(2,1)} %param.12), kind=kOutput, calls=%fused_computation.8 | convolution fusion | flops 3238395904 | bytes 20709376 | tf_op jit(solution)/shard_map/dot_general | solution.py:127
  369.8 2.3 copy.26
  (7 shorter events, 0.1 us)
Async XLA Ops:
  7.2 241.8 %reduce-scatter.3.cloned.1.call-start = ((), (), s32[]{:S(2)}) async-start(), calls=%async_computation.2 | async-start | bytes 9437184 | tf_op jit(solution)/shard_map/reduce_scatter | solution.py:102
  55.0 13.3 %copy-start.2 = (s32[1,8,32]{2,1,0:T(8,128)S(1)}, s32[1,8,32]{2,1,0:T(8,128)}, u32[]{:S(2)}) copy-start(s32[1,8,32]{2,1,0:T(8,128)} %param.15) | copy-start | bytes 3076
  68.4 23.5 %slice-start = ((s8[8388608]{0:T(1024)(128)(4,1)}), s8[4194304]{0:T(1024)(128)(4,1)S(1)}, s32[]{:S(2)}) async-start(s8[8388608]{0:T(1024)(128)(4,1)} %bitcast.49), calls=%async_computation.5 | async-start | bytes 8388608
  80.2 11.8 %slice-start.1 = ((s8[8388608]{0:T(1024)(128)(4,1)}), s8[4194304]{0:T(1024)(128)(4,1)S(1)}, s32[]{:S(2)}) async-start(s8[8388608]{0:T(1024)(128)(4,1)} %bitcast.49), calls=%async_computation.6 | async-start | bytes 8388608
  98.6 150.5 %copy-start.1 = (s32[32,32]{1,0:T(8,128)S(1)}, s32[32,32]{1,0:T(8,128)}, u32[]{:S(2)}) copy-start(s32[32,32]{1,0:T(8,128)} %param.16) | copy-start | bytes 12292
  98.6 262.0 %copy-start = (bf16[384,4096]{1,0:T(8,128)(2,1)S(1)}, bf16[384,4096]{1,0:T(8,128)(2,1)}, u32[]{:S(2)}) copy-start(bf16[384,4096]{1,0:T(8,128)(2,1)} %param.9) | copy-start | bytes 9437188
  98.6 176.8 %reduce-scatter.5.cloned.1.call-start = ((), (), s32[]{:S(2)}) async-start(), calls=%async_computation.3 | async-start | bytes 1310720 | tf_op jit(solution)/shard_map/reduce_scatter | solution.py:111
  249.0 111.6 %all-gather.2.cloned.1.call-start = ((), (), s32[]{:S(2)}) async-start(), calls=%async_computation.4 | async-start | bytes 8650752 | tf_op jit(solution)/shard_map/all_gather | solution.py:125
Sparse Core Ops, SparseCore 0:
  98.7 150.1 reduce-scatter.2
  251.5 23.8 reduce-scatter.4
  283.5 77.0 all-gather.1
where the time goes:
time: 379 us
  waiting for transfers between devices  254 us (67%)
  local copies, waits for them, and re-layouts  69.6 us (18%)
  matrix products  30.4 us (8%)
  between operations  13.9 us (4%)
  other arithmetic  10.7 us (3%)
    reduce_scatter x1, waiting for transfers between devices, shards(): lax.psum_scatter(coded_rows.reshape(1 * lax.axis_size('inner'), outer_cou...  150 us
    all_gather x1, waiting for transfers between devices, shards(): lax.all_gather(diff_coded, ('outer', 'inner'), axis=0, tiled=True)  77.2 us
    reduce_scatter x1, waiting for transfers between devices, shards(): lax.psum_scatter(group_sum, 'outer', scatter_dimension=1, tiled=True)  26.3 us
    mul x1, local copies, waits for them, and re-layouts, rotate_rows(): row_block.reshape(row_count, sign_rows.shape[0], sign_rows.shape[1])  20.2 us
    dot_general x1, matrix products, rotate_rows(): jnp.dot(blocks.reshape(-1, sign_rows.shape[1]), matrix, precision=highest)  15.3 us
    div x1, local copies, waits for them, and re-layouts, rotate_rows(): return turned.reshape(row_block.shape) / math.sqrt(sign_rows.shape[1])  13.3 us
    max x2, local copies, waits for them, and re-layouts, clip_rows(): return jnp.clip(shaped, -limits, limits).reshape(row_block.shape)  11.9 us
    min x2, local copies, waits for them, and re-layouts, clip_rows(): return jnp.clip(shaped, -limits, limits).reshape(row_block.shape)  11.9 us
  transfers between devices with their start and end apart: 3, of which 3 were waited for; matrix products, arithmetic and copies ran while one was open for 0% of the time, Pallas kernels for 0%

commit v1 on v0

--- a/solution.py
+++ b/solution.py
@@ -1,8 +1,11 @@
+import functools
 import math
 
 import jax
 import jax.numpy as jnp
 from jax import lax
+from jax.experimental import pallas as pl
+from jax.experimental.pallas import tpu as pltpu
 from jax.sharding import PartitionSpec as P
 
 ADAM_STEP = 10
@@ -58,6 +61,345 @@
     step_dir = new_first / fix_one / (jnp.sqrt(new_second / fix_two) + adam_eps)
     new_master = master - learn_rate * (step_dir + decay_rate * master)
     return (new_master, new_first, new_second)
+
+
+CHUNKS = 8
+MESH = pl.DeviceIdType.MESH
+
+
+def step_kernel(
+    chunks,
+    tokens,
+    grad_t,
+    master,
+    base_hbm,
+    first,
+    second,
+    bounds,
+    diff_bounds,
+    signs,
+    matrix_half,
+    matrix,
+    projected,
+    out_master,
+    out_first,
+    out_second,
+    base,
+    coded,
+    rec0,
+    sum0,
+    rec1,
+    sum1,
+    rec2,
+    sum2,
+    rec3,
+    gath,
+    turned,
+    effective,
+    total,
+    base_sem,
+    send_sem,
+    recv_sem,
+    zsend,
+    zrecv,
+):
+    outer, inner = lax.axis_index("outer"), lax.axis_index("inner")
+    inner_count = lax.axis_size("inner")
+    xs = 2
+    zs = inner_count // xs
+    y, c = outer // 2, outer % 2
+    z, x = inner // xs, inner % xs
+    rows = master.shape[0]
+    width = tokens.shape[1] // chunks
+    block_len = matrix.shape[0]
+    blocks = width // block_len
+    row_blocks = grad_t.shape[0] // block_len
+    z_step = block_len // (xs * rows)
+    scale = 1.0 / math.sqrt(block_len)
+    mine1 = x * (1 - c) + y * c
+    mine2 = y * (1 - c) + x * c
+    core_peer = (y * 2 + 1 - c, inner)
+    x_peer = (outer, z * xs + 1 - x)
+    y_peer = ((1 - y) * 2 + c, inner)
+    peer1 = (x_peer[0] * (1 - c) + y_peer[0] * c, x_peer[1] * (1 - c) + y_peer[1] * c)
+    peer2 = (y_peer[0] * (1 - c) + x_peer[0] * c, y_peer[1] * (1 - c) + x_peer[1] * c)
+    z_ids = [lax.rem(z + k, zs) for k in range(1, zs)]
+    z_peers = [(outer, zz * xs + x) for zz in z_ids]
+
+    load_base = pltpu.make_async_copy(base_hbm, base, base_sem)
+    load_base.start()
+    barrier = pltpu.get_barrier_semaphore()
+    peers = [core_peer, peer1, peer2] + z_peers
+    for peer in peers:
+        pl.semaphore_signal(barrier, inc=1, device_id=peer, device_id_type=MESH)
+    total[...] = jnp.zeros_like(total)
+    pl.semaphore_wait(barrier, len(peers))
+
+    def remote(src, dst, stage, j, peer):
+        return pltpu.make_async_remote_copy(
+            src_ref=src,
+            dst_ref=dst,
+            send_sem=send_sem.at[stage, j],
+            recv_sem=recv_sem.at[stage, j],
+            device_id=peer,
+            device_id_type=MESH,
+        )
+
+    def remote_z(src, dst, stage, j, k):
+        return pltpu.make_async_remote_copy(
+            src_ref=src,
+            dst_ref=dst,
+            send_sem=zsend.at[stage, j, k],
+            recv_sem=zrecv.at[stage, j, k],
+            device_id=z_peers[k],
+            device_id_type=MESH,
+        )
+
+    def copy0(j):
+        return remote(coded.at[j, 1 - c], rec0.at[j], 0, j, core_peer)
+
+    def copy1(j):
+        return remote(sum0.at[j, 1 - mine1], rec1.at[j], 1, j, peer1)
+
+    def copy2(j):
+        return remote(sum1.at[j, 1 - mine2], rec2.at[j], 2, j, peer2)
+
+    def copy3(j):
+        return [remote_z(sum2.at[j, z_ids[k]], rec3.at[j, k], 0, j, k) for k in range(zs - 1)]
+
+    def gather0(j):
+        block = gath.at[j, c, mine1, mine2, z]
+        return [remote_z(block, block, 1, j, k) for k in range(zs - 1)]
+
+    def gather1(j):
+        block = gath.at[j, c, mine1, mine2]
+        return remote(block, block, 3, j, peer2)
+
+    def gather2(j):
+        block = gath.at[j, c, mine1]
+        return remote(block, block, 4, j, peer1)
+
+    def gather3(j):
+        block = gath.at[j, c]
+        return remote(block, block, 5, j, core_peer)
+
+    def added(left, right):
+        return (left.astype(jnp.float32) + right.astype(jnp.float32)).astype(jnp.bfloat16)
+
+    def columns(j):
+        return pl.ds(pl.multiple_of(j * width, width), width)
+
+    def produce(j):
+        for b in range(blocks):
+            at = pl.ds(pl.multiple_of(j * width + b * block_len, block_len), block_len)
+            part = jnp.dot(
+                tokens[:, at] * signs[:, at].astype(jnp.bfloat16),
+                matrix_half[...],
+                preferred_element_type=jnp.float32,
+            )
+            turned[:, b * block_len : (b + 1) * block_len] = (part * scale).astype(jnp.bfloat16)
+
+        def one(m, carry):
+            part = jnp.dot(
+                grad_t[pl.ds(pl.multiple_of(m * block_len, block_len), block_len), :],
+                turned[...],
+                preferred_element_type=jnp.float32,
+            )
+            limit = bounds[pl.ds(m, 1), columns(j)]
+            part = jnp.minimum(jnp.maximum(part, -limit), limit).astype(jnp.bfloat16)
+            per = row_blocks // 4
+            group = m // per
+            z0 = (m - group * per) * z_step
+            coded[j, group % 2, group // 2, pl.ds(z0, z_step)] = part.reshape(
+                z_step, xs, rows, width
+            )
+            return carry
+
+        lax.fori_loop(0, row_blocks, one, 0)
+        copy0(j).start()
+
+    def reduce0(j):
+        copy0(j).wait()
+        for yy in range(2):
+            for zz in range(zs):
+                for xx in range(xs):
+                    to1 = xx * (1 - c) + yy * c
+                    to2 = yy * (1 - c) + xx * c
+                    sum0[j, to1, to2, zz] = added(coded[j, c, yy, zz, xx], rec0[j, yy, zz, xx])
+        copy1(j).start()
+
+    def reduce1(j):
+        copy1(j).wait()
+        sum1[j] = added(sum0[j, mine1], rec1[j])
+        copy2(j).start()
+
+    def reduce2(j):
+        copy2(j).wait()
+        sum2[j] = added(sum1[j, mine2], rec2[j])
+        for item in copy3(j):
+            item.start()
+
+    def update(j):
+        copies = copy3(j)
+        for item in copies:
+            item.wait()
+        summed = sum2[j, z].astype(jnp.float32)
+        for k in range(zs - 1):
+            summed = summed + rec3[j, k].astype(jnp.float32)
+        own = pl.ds(pl.multiple_of((outer * inner_count + inner) * rows, rows), rows)
+        for b in range(blocks):
+            at = pl.ds(pl.multiple_of(j * width + b * block_len, block_len), block_len)
+            gradient = (
+                jnp.dot(
+                    summed[:, b * block_len : (b + 1) * block_len],
+                    matrix[...],
+                    precision=highest,
+                    preferred_element_type=jnp.float32,
+                )
+                * scale
+                * signs[:, at]
+            )
+            new_master, new_first, new_second = adam_update(
+                gradient, master[:, at], first[:, at], second[:, at]
+            )
+            out_master[:, at] = new_master
+            out_first[:, at] = new_first
+            out_second[:, at] = new_second
+            limit = diff_bounds[j, :, b : b + 1]
+            change = new_master - base[own, at].astype(jnp.float32)
+            change = jnp.minimum(jnp.maximum(change, -limit), limit)
+            gath[j, c, mine1, mine2, z, :, b * block_len : (b + 1) * block_len] = change.astype(
+                jnp.bfloat16
+            )
+        for item in gather0(j):
+            item.start()
+
+    def pass1(j):
+        for item in gather0(j):
+            item.wait()
+        gather1(j).start()
+
+    def pass2(j):
+        gather1(j).wait()
+        gather2(j).start()
+
+    def pass3(j):
+        gather2(j).wait()
+        gather3(j).start()
+
+    def consume(j):
+        gather3(j).wait()
+        for yy in range(2):
+            for cc in range(2):
+                group = yy * 2 + cc
+                count = zs * xs * rows
+                for zz in range(zs):
+                    for xx in range(xs):
+                        at1, at2 = (xx, yy) if cc == 0 else (yy, xx)
+                        low = (zz * xs + xx) * rows
+                        effective[low : low + rows, :] = added(
+                            base[group * count + low : group * count + low + rows, columns(j)],
+                            gath[j, cc, at1, at2, zz],
+                        )
+                total[:, group * count : (group + 1) * count] += lax.dot_general(
+                    tokens[:, columns(j)],
+                    effective[...],
+                    (((1,), (1,)), ((), ())),
+                    preferred_element_type=jnp.float32,
+                )
+
+    stages = (produce, reduce0, reduce1, reduce2, update, pass1, pass2, pass3, consume)
+
+    def step(t, carry):
+        for place, stage in enumerate(stages):
+            j = t - place
+
+            @pl.when((j >= 0) & (j < chunks))
+            def _():
+                stage(j)
+
+        return carry
+
+    lax.fori_loop(0, 4, step, 0)
+    load_base.wait()
+    lax.fori_loop(4, chunks + len(stages) - 1, step, 0)
+    projected[...] = total[...].astype(jnp.bfloat16)
+
+
+def fused_step(tokens, out_grad, master, base, first, second, bounds, diff_bounds, signs, matrix):
+    rows, model_width = master.shape
+    features = out_grad.shape[1]
+    inner_count = lax.axis_size("inner")
+    zs = inner_count // 2
+    width = model_width // CHUNKS
+    vmem = pl.BlockSpec(memory_space=pltpu.VMEM)
+    half = jnp.bfloat16
+    cell = (rows, width)
+    flops = 4 * tokens.shape[0] * model_width * features
+    return pl.pallas_call(
+        functools.partial(step_kernel, CHUNKS),
+        out_shape=(
+            jax.ShapeDtypeStruct((tokens.shape[0], features), half),
+            jax.ShapeDtypeStruct(master.shape, jnp.float32),
+            jax.ShapeDtypeStruct(master.shape, jnp.float32),
+            jax.ShapeDtypeStruct(master.shape, jnp.float32),
+        ),
+        in_specs=[vmem] * 3 + [pl.BlockSpec(memory_space=pl.ANY)] + [vmem] * 7,
+        out_specs=(vmem,) * 4,
+        scratch_shapes=[
+            pltpu.VMEM(base.shape, half),
+            pltpu.VMEM((CHUNKS, 2, 2, zs, 2) + cell, half),
+            pltpu.VMEM((CHUNKS, 2, zs, 2) + cell, half),
+            pltpu.VMEM((CHUNKS, 2, 2, zs) + cell, half),
+            pltpu.VMEM((CHUNKS, 2, zs) + cell, half),
+            pltpu.VMEM((CHUNKS, 2, zs) + cell, half),
+            pltpu.VMEM((CHUNKS, zs) + cell, half),
+            pltpu.VMEM((CHUNKS, zs) + cell, half),
+            pltpu.VMEM((CHUNKS, zs - 1) + cell, half),
+            pltpu.VMEM((CHUNKS, 2, 2, 2, zs) + cell, half),
+            pltpu.VMEM((tokens.shape[0], width), half),
+            pltpu.VMEM((features // 4, width), half),
+            pltpu.VMEM((tokens.shape[0], features), jnp.float32),
+            pltpu.SemaphoreType.DMA,
+            pltpu.SemaphoreType.DMA((6, CHUNKS)),
+            pltpu.SemaphoreType.DMA((6, CHUNKS)),
+            pltpu.SemaphoreType.DMA((2, CHUNKS, zs - 1)),
+            pltpu.SemaphoreType.DMA((2, CHUNKS, zs - 1)),
+        ],
+        compiler_params=pltpu.CompilerParams(
+            collective_id=0, has_side_effects=True, vmem_limit_bytes=66000000
+        ),
+        cost_estimate=pl.CostEstimate(flops=flops, bytes_accessed=2**25, transcendentals=0),
+    )(
+        tokens,
+        out_grad.T,
+        master,
+        base,
+        first,
+        second,
+        bounds,
+        diff_bounds,
+        signs,
+        matrix.astype(half),
+        matrix,
+    )
+
+
+def fits_kernel(token_rows, rows_dev, block_len, features, model_width):
+    inner_count = lax.axis_size("inner")
+    pair = 2 * rows_dev
+    return (
+        lax.axis_size("outer") == 4
+        and inner_count % 2 == 0
+        and inner_count > 2
+        and rows_dev % 16 == 0
+        and token_rows % 16 == 0
+        and block_len % pair == 0
+        and (inner_count * rows_dev) % block_len == 0
+        and features == 4 * inner_count * rows_dev
+        and model_width % (CHUNKS * block_len) == 0
+        and features * model_width <= 2**22
+    )
 
 
 def shards(
@@ -83,6 +425,21 @@
     bound_all = jnp.repeat(
         clip_level * jnp.exp2(grad_exps[0].astype(jnp.float32)), block_len, axis=0
     )
+    if fits_kernel(token_rows, rows_dev, block_len, out_grad.shape[1], model_width):
+        limits = clip_level * jnp.exp2(grad_exps[0].astype(jnp.float32))
+        diff_limits = clip_level * jnp.exp2(diff_exps.astype(jnp.float32))
+        return fused_step(
+            tokens,
+            out_grad,
+            master_weights,
+            base_weights,
+            adam_m,
+            adam_v,
+            jnp.repeat(limits, block_len, axis=1),
+            diff_limits.reshape(rows_dev, CHUNKS, -1).transpose(1, 0, 2),
+            sign_rows.reshape(1, -1),
+            matrix,
+        )
     grad_grid = out_grad.reshape(token_rows, outer_count, inner_count, rows_dev).transpose(
         0, 2, 1, 3
     )

time: 379 us -> 108 us (0.28)
  waiting for transfers between devices: 254 us -> 0 us
  Pallas kernels: 0 us -> 91.5 us
  local copies, waits for them, and re-layouts: 69.6 us -> 12.4 us
  matrix products: 30.4 us -> 0 us
  between operations: 13.9 us -> 0.65 us
  other arithmetic: 10.7 us -> 2.75 us
    reduce_scatter x2 -> x0, waiting for transfers between devices: 177 us -> none  [the longest x1 150 us: shards(): lax.psum_scatter(coded_rows.reshape(1 * lax.axis_size('inner'), outer_cou...]
    pallas_call x0 -> x1, Pallas kernels: none -> 91.5 us  [fused_step(): pl.pallas_call(functools.partial(step_kernel, CHUNKS), out_shape=(jax.Sha...]
    all_gather x1 -> x0, waiting for transfers between devices: 77.2 us -> none  [shards(): lax.all_gather(diff_coded, ('outer', 'inner'), axis=0, tiled=True)]
    dot_general x4 -> x0, matrix products: 30.4 us -> none  [the longest x1 15.3 us: rotate_rows(): jnp.dot(blocks.reshape(-1, sign_rows.shape[1]), matrix, precision=highest)]
    mul x1, local copies, waits for them, and re-layouts: 20.2 us -> 0.08 us  [shards(): limits = clip_level * jnp.exp2(grad_exps[0].astype(jnp.float32))]
    div x1 -> x0, local copies, waits for them, and re-layouts: 13.3 us -> none  [rotate_rows(): return turned.reshape(row_block.shape) / math.sqrt(sign_rows.shape[1])]
    max x2 -> x0, local copies, waits for them, and re-layouts: 11.9 us -> none  [clip_rows(): return jnp.clip(shaped, -limits, limits).reshape(row_block.shape)]
    min x2 -> x0, local copies, waits for them, and re-layouts: 11.9 us -> none  [clip_rows(): return jnp.clip(shaped, -limits, limits).reshape(row_block.shape)]
  transfers between devices with their start and end apart: 3 -> 0, of which waited for: 3 -> 0; matrix products, arithmetic and copies ran while one was open for 0% -> 0% of each run, Pallas kernels for 0% -> 0%
where the time goes in v1:
time: 108 us; the launch traced here: 107 us
  Pallas kernels  91.5 us (85%)
  local copies, waits for them, and re-layouts  12.4 us (11%)
  other arithmetic  2.75 us (3%)
    pallas_call x1, Pallas kernels, fused_step(): pl.pallas_call(functools.partial(step_kernel, CHUNKS), out_shape=(jax.Sha...  91.5 us
    unnamed x6, local copies, waits for them, and re-layouts  10.7 us

profile of v1, /device:TPU:0, one launch (start us, length us, event | category | flops | bytes accessed | tf_op | source)
XLA Modules:
  0.0 107.2 jit_solution(2057319076017448042)
XLA Ops:
  0.6 0.7 multiply_bitcast_fusion
  1.3 0.1 copy.16
  1.4 0.8 copy.17
  2.2 1.3 %add_convert_fusion = f32[32,128]{1,0:T(8,128)} fusion(s32[32,128]{1,0:T(8,128)} %param.17), kind=kLoop, calls=%fused_computation.9 | loop fusion | flops 12288 | bytes 32768 | tf_op jit(solution)/shard_map/convert_element_type | solution.py:421
  3.5 0.7 fusion.3
  4.3 0.8 copy.18
  5.0 0.8 broadcast_bitcast_fusion.bounds
  5.8 2.3 %copy.15 = bf16[384,1024]{0,1:T(8,128)(2,1)} copy(bf16[384,1024]{1,0:T(8,128)(2,1)} %param.10) | data formatting | bytes 1572864 | tf_op args[1]
  8.1 91.5 %shard_map.120 = (bf16[384,1024]{1,0:T(8,128)(2,1)}, f32[32,4096]{1,0:T(8,128)}, f32[32,4096]{1,0:T(8,128)}, f32[32,4096]{1,0:T(8,128)}) custom-call(bf16[384,4096]{1,0:T(8,128)(2,1)} %tokens.1, bf16[1024,384]{1,0:T(8,128)(2,1)} %bitcast.8, f32[32,4096]{1,0:T(8,128)} %master.1, bf16[1024,4096]{1,0:T(8,128)(2,1)} %base_hbm.1, f32[32,4096]{1,0:T(8,128)} %first.1, ...), custom_call_target="tpu_custom_call" | custom-call | flops 6442450944 | bytes 33554432 | tf_op jit(solution)/shard_map/pallas_call | solution.py:339
  99.6 2.1 %copy.23 = bf16[384,1024]{1,0:T(8,128)(2,1)} copy(bf16[384,1024]{1,0:T(8,128)(2,1)} %get-tuple-element.10) | data formatting | bytes 1572864
  101.6 1.9 %copy.24 = f32[32,4096]{1,0:T(8,128)} copy(f32[32,4096]{1,0:T(8,128)} %get-tuple-element.11) | data formatting | bytes 1048576
  103.5 1.9 %copy.25 = f32[32,4096]{1,0:T(8,128)} copy(f32[32,4096]{1,0:T(8,128)} %get-tuple-element.12) | data formatting | bytes 1048576
  105.4 1.9 %copy.26 = f32[32,4096]{1,0:T(8,128)} copy(f32[32,4096]{1,0:T(8,128)} %get-tuple-element.13) | data formatting | bytes 1048576
  (1 shorter events, 0.0 us)
